TPU v7x, 32 devices: a whole 2x2x4 slice. The times are simulated.
32 devices in a mesh: rep: 4 (over x, y), dp: 8 (over z, core).
Axes of the slice: x: 2, y: 2, z: 4, core: 2. Of those that a mesh axis runs over, the one named last changes fastest.
Arguments:
- x: bfloat16 [32, 2048, 640], P(('rep', 'dp')), parts along dimension 0
- dy: bfloat16 [32, 2048, 640], P(('rep', 'dp')), parts along dimension 0
- w_gate: bfloat16 [2, 640, 2048], replicated
- w_up: bfloat16 [2, 640, 2048], replicated
- w_down: bfloat16 [2, 2048, 640], replicated
- m_w_gate: float32 [2, 640, 2048], replicated
- m_w_up: float32 [2, 640, 2048], replicated
- m_w_down: float32 [2, 2048, 640], replicated
- v_w_gate: float32 [2, 640, 2048], replicated
- v_w_up: float32 [2, 640, 2048], replicated
- v_w_down: float32 [2, 2048, 640], replicated
Outputs:
- output 1: bfloat16 [8, 640, 2048], P('rep'), parts along dimension 0
- output 2: bfloat16 [8, 640, 2048], P('rep'), parts along dimension 0
- output 3: bfloat16 [8, 2048, 640], P('rep'), parts along dimension 0
- output 4: float32 [8, 640, 2048], P('rep'), parts along dimension 0
- output 5: float32 [8, 640, 2048], P('rep'), parts along dimension 0
- output 6: float32 [8, 2048, 640], P('rep'), parts along dimension 0
- output 7: float32 [8, 640, 2048], P('rep'), parts along dimension 0
- output 8: float32 [8, 640, 2048], P('rep'), parts along dimension 0
- output 9: float32 [8, 2048, 640], P('rep'), parts along dimension 0
There are 4 independent parts. A program takes and returns all parts, laid end to end along the dimension named above; an argument that names none is the same for every part.
All inputs are finite; a program needn't handle non-finite values.
Results may differ from a plain program's by a relative error of at most 0.022.
Values are sent between devices in bfloat16 or wider.
A program may use at most 2.25 GiB of HBM per device.

v0:
```python
import jax
import jax.numpy as jnp
from jax import lax
from jax.sharding import PartitionSpec as P

NAMES = ("w_gate", "w_up", "w_down")


def matmul(a, w):
    return jnp.dot(a, w, preferred_element_type=jnp.float32).astype(jnp.bfloat16)


def normed(h):
    wide = h.astype(jnp.float32)
    scale = lax.rsqrt(jnp.mean(wide**2, -1, keepdims=True) + 1e-6)
    return (wide * scale).astype(jnp.bfloat16)


def layer(h, w):
    a = normed(h)
    gate = jnp.dot(a, w["w_gate"], preferred_element_type=jnp.float32)
    up = jnp.dot(a, w["w_up"], preferred_element_type=jnp.float32)
    return h + matmul((jax.nn.silu(gate) * up).astype(jnp.bfloat16), w["w_down"])


def adamw(w, m, v, g):
    m = 0.9 * m + 0.1 * g
    v = 0.95 * v + 0.05 * g * g
    step = m * lax.rsqrt(v + 1e-8) + 0.1 * w
    return (w - 0.02 * step).astype(jnp.bfloat16), m, v


def solution(mesh):
    def step(x, dy, *arrays):
        weights, m, v = (arrays[i : i + 3] for i in (0, 3, 6))
        layers = weights[0].shape[0]
        h, kept = x[0], []
        for number in range(layers):
            kept.append(h)
            h = layer(h, {name: w[number] for name, w in zip(NAMES, weights, strict=True)})
        by_h, summed = dy[0], [None] * layers
        for number in reversed(range(layers)):
            _, back = jax.vjp(lambda w, h: layer(h, w), {name: w[number] for name, w in zip(NAMES, weights, strict=True)}, kept[number])
            by_w, by_h = back(by_h)
            summed[number] = [lax.psum(by_w[name], "dp") for name in NAMES]
        gradients = [jnp.stack([summed[number][i] for number in range(layers)]).astype(jnp.float32) for i in range(3)]
        new = [adamw(w.astype(jnp.float32), m, v, g) for w, m, v, g in zip(weights, m, v, gradients, strict=True)]
        return tuple(one[which] for which in range(3) for one in new)

    return jax.shard_map(
        step,
        mesh=mesh,
        in_specs=(P(("rep", "dp"), None, None),) * 2 + (P(None, None, None),) * 9,
        out_specs=(P("rep", None, None),) * 9,
        check_vma=False,
    )
```

profile of v0, /device:TPU:0, one launch (start us, length us, event | category | flops | bytes accessed | tf_op | source)
XLA Modules:
  0.0 599.3 jit_solution(16734714037650018623)
XLA Ops:
  7.2 0.0 all-reduce.3.cloned.1.call-start
  7.2 3.0 copy.20
  10.2 0.6 fusion.30
  10.8 4.7 copy.21
  15.5 11.3 %convolution_convert_fusion.1 = bf16[2048,2048]{1,0:T(8,128)(2,1)} fusion(bf16[1,2048,640]{2,1,0:T(8,128)(2,1)} %param.12, bf16[2,2048,640]{2,1,0:T(8,128)(2,1)} %param.15), kind=kOutput, calls=%fused_computation.56 | convolution fusion | flops 5372903424 | bytes 13631488 | tf_op jit(solution)/shard_map/transpose(jvp())/dot_general | solution.py:10
  26.8 11.6 %fusion.68 = f32[2048,2048]{1,0:T(8,128)} fusion(bf16[2,640,2048]{2,1,0:T(8,128)(2,1)} %param.13, bf16[1,2048,640]{2,1,0:T(8,128)(2,1)S(1)} %copy-done.5, f32[2048]{0:T(1024)S(1)} %add_rsqrt_fusion), kind=kOutput, calls=%fused_computation.101 | convolution fusion | flops 5372641280 | bytes 22028288 | tf_op jit(solution)/shard_map/dot_general | solution.py:21
  38.4 16.9 %multiply_convert_fusion.1 = (bf16[2048,2048]{1,0:T(8,128)(2,1)}, f32[2048,2048]{1,0:T(8,128)}) fusion(f32[2048,2048]{1,0:T(8,128)} %fusion.68, bf16[2,640,2048]{2,1,0:T(8,128)(2,1)} %param.14, bf16[1,2048,640]{2,1,0:T(8,128)(2,1)} %param.11, f32[2048]{0:T(1024)S(1)} %add_rsqrt_fusion), kind=kOutput, calls=%fused_computation.17 | convolution fusion | flops 5397807104 | bytes 47194112 | tf_op jit(solution)/shard_map/dot_general | solution.py:22
  55.3 9.2 %fusion.34 = (f32[2048]{0:T(1024)S(1)}, bf16[2048,640]{0,1:T(8,128)(2,1)S(1)}) fusion(bf16[2048,2048]{1,0:T(8,128)(2,1)} %get-tuple-element.24, bf16[2,2048,640]{2,1,0:T(8,128)(2,1)} %param.15, bf16[1,2048,640]{1,2,0:T(8,128)(2,1)S(1)} %copy.20), kind=kOutput, calls=%fused_computation.64 | convolution fusion | flops 5375260672 | bytes 16261120 | tf_op jit(solution)/shard_map/dot_general | solution.py:10
  64.5 1.5 copy-done.3
  65.9 12.2 %fusion.57 = f32[2048,2048]{1,0:T(8,128)} fusion(bf16[2,640,2048]{2,1,0:T(8,128)(2,1)} %param.14, bf16[2048,640]{0,1:T(8,128)(2,1)S(1)} %get-tuple-element.27, f32[2048]{0:T(1024)S(1)} %fusion.92), kind=kOutput, calls=%fused_computation.90 | convolution fusion | flops 5372641280 | bytes 22028288 | tf_op jit(solution)/shard_map/jvp()/dot_general | solution.py:22
  78.1 25.1 %fusion.2 = (bf16[2048,2048]{1,0:T(8,128)(2,1)}, f32[2048,2048]{1,0:T(8,128)}) fusion(f32[2048,2048]{1,0:T(8,128)} %fusion.57, bf16[2048,2048]{1,0:T(8,128)(2,1)} %convolution_convert_fusion.1, bf16[2,640,2048]{2,1,0:T(8,128)(2,1)} %param.13, bf16[2048,640]{0,1:T(8,128)(2,1)} %copy-done.3, f32[2048]{0:T(1024)S(1)} %fusion.92), kind=kOutput, calls=%fused_computation.8 | convolution fusion | flops 5422972928 | bytes 55582720 | tf_op jit(solution)/shard_map/jvp()/dot_general | solution.py:21
  103.2 16.9 %fusion.49 = bf16[1,2048,640]{2,1,0:T(8,128)(2,1)} fusion(f32[2048,2048]{1,0:T(8,128)} %fusion.57, bf16[1,2048,640]{2,1,0:T(8,128)(2,1)} %param.12, f32[2048,2048]{1,0:T(8,128)} %get-tuple-element.29), kind=kOutput, calls=%fused_computation.82 | convolution fusion | flops 5395185664 | bytes 38797312 | tf_op jit(solution)/shard_map/transpose(jvp())/dot_general | solution.py:10
  120.2 13.3 %fusion.52 = bf16[1,640,2048]{2,1,0:T(8,128)(2,1)} fusion(bf16[2048,2048]{1,0:T(8,128)(2,1)} %convolution_convert_fusion.1, bf16[2048,640]{0,1:T(8,128)(2,1)} %copy-done.3, f32[2048]{0:T(1024)S(1)} %fusion.92, f32[2048,2048]{1,0:T(8,128)} %get-tuple-element.29), kind=kOutput, calls=%fused_computation.85 | convolution fusion | flops 5399117824 | bytes 30416896 | tf_op jit(solution)/shard_map/transpose(jvp())/dot_general | solution.py:22
  133.5 12.4 %fusion.38 = bf16[2048,640]{0,1:T(8,128)(2,1)} fusion(bf16[2048,2048]{1,0:T(8,128)(2,1)} %convolution_convert_fusion.1, bf16[2,640,2048]{2,1,0:T(8,128)(2,1)S(1)} %bitcast.77, f32[2048,2048]{1,0:T(8,128)} %get-tuple-element.29), kind=kOutput, calls=%fused_computation.72 | convolution fusion | flops 5395185664 | bytes 30408704 | tf_op jit(solution)/shard_map/transpose(jvp())/dot_general | solution.py:22
  145.9 10.9 %fusion.50 = bf16[1,640,2048]{2,1,0:T(8,128)(2,1)} fusion(bf16[2048,2048]{1,0:T(8,128)(2,1)} %get-tuple-element.28, bf16[2048,640]{0,1:T(8,128)(2,1)} %copy-done.3, f32[2048]{0:T(1024)S(1)} %fusion.92), kind=kOutput, calls=%fused_computation.83 | convolution fusion | flops 5372641280 | bytes 13639680 | tf_op jit(solution)/shard_map/transpose(jvp())/dot_general | solution.py:21
  156.9 8.5 %fusion.36 = (f32[2048]{0:T(1024)S(1)}, bf16[2048,640]{0,1:T(8,128)(2,1)S(1)}) fusion(bf16[2048,640]{0,1:T(8,128)(2,1)S(1)} %copy-done.4, bf16[2048,640]{0,1:T(8,128)(2,1)S(1)} %copy-done.12, bf16[2048,2048]{1,0:T(8,128)(2,1)} %get-tuple-element.28, bf16[2,640,2048]{2,1,0:T(8,128)(2,1)S(1)} %bitcast.75), kind=kOutput, calls=%fused_computation.66 | convolution fusion | flops 5375260672 | bytes 18882560 | tf_op jit(solution)/shard_map/transpose(jvp())/dot_general | solution.py:21
  165.4 2.0 fusion.54
  167.5 10.5 %fusion.51 = bf16[1,2048,640]{2,1,0:T(8,128)(2,1)} fusion(bf16[2048,2048]{1,0:T(8,128)(2,1)} %get-tuple-element.24, bf16[2048,640]{0,1:T(8,128)(2,1)S(1)} %fusion.54), kind=kOutput, calls=%fused_computation.84 | convolution fusion | flops 5370019840 | bytes 13631488 | tf_op jit(solution)/shard_map/transpose(jvp())/dot_general | solution.py:10
  178.0 7.3 %convolution_convert_fusion = bf16[2048,2048]{1,0:T(8,128)(2,1)S(1)} fusion(bf16[2048,640]{0,1:T(8,128)(2,1)S(1)} %fusion.54, bf16[2,2048,640]{2,1,0:T(8,128)(2,1)S(1)} %bitcast.79), kind=kOutput, calls=%fused_computation.55 | convolution fusion | flops 5372903424 | bytes 13631488 | tf_op jit(solution)/shard_map/transpose(jvp())/dot_general | solution.py:10
  185.3 13.9 %fusion.45 = bf16[1,640,2048]{2,1,0:T(8,128)(2,1)} fusion(bf16[2048,2048]{1,0:T(8,128)(2,1)S(1)} %convolution_convert_fusion, f32[2048,2048]{1,0:T(8,128)} %fusion.68, bf16[1,2048,640]{1,2,0:T(8,128)(2,1)S(1)} %copy-done.2, f32[2048]{0:T(1024)S(1)} %copy-done.10), kind=kOutput, calls=%fused_computation.80 | convolution fusion | flops 5399117824 | bytes 30416896 | tf_op jit(solution)/shard_map/transpose(jvp())/dot_general | solution.py:22
  199.2 19.0 %fusion.46 = bf16[1,640,2048]{2,1,0:T(8,128)(2,1)} fusion(f32[2048,2048]{1,0:T(8,128)} %fusion.68, f32[2048,2048]{1,0:T(8,128)} %get-tuple-element.25, bf16[2048,2048]{1,0:T(8,128)(2,1)} %copy-done.11, bf16[1,2048,640]{1,2,0:T(8,128)(2,1)S(1)} %copy-done.2, f32[2048]{0:T(1024)S(1)} %copy-done.10), kind=kOutput, calls=%fused_computation.81 | convolution fusion | flops 5420089344 | bytes 47194112 | tf_op jit(solution)/shard_map/transpose(jvp())/dot_general | solution.py:21
  218.2 316.6 %all-reduce.3.cloned.1.call-done = (bf16[1,640,2048]{2,1,0:T(8,128)(2,1)}, bf16[1,640,2048]{2,1,0:T(8,128)(2,1)}, bf16[1,640,2048]{2,1,0:T(8,128)(2,1)}, bf16[1,...) async-done(((bf16[1,640,2048]{2,1,0:T(8,128)(2,1)}, bf16[1,640,2048]{2,1,0:T(8,128)(2,1)}, bf16[1,640,2048]{2,1,0:T(8,128)(2,1)}, ...) | async-done | bytes 15728656 | tf_op jit(solution)/shard_map/psum | solution.py:45
  534.9 22.1 %fusion.23 = (bf16[2,2048,640]{2,1,0:T(8,128)(2,1)}, f32[2,2048,640]{2,1,0:T(8,128)}, f32[2,2048,640]{2,1,0:T(8,128)}) fusion(bf16[2,2048,640]{2,1,0:T(8,128)(2,1)} %param.15, bf16[1,2048,640]{2,1,0:T(8,128)(2,1)} %get-tuple-element.13, bf16[1,2048,640]{2,1,0:T(8,128)(2,1)} %get-tuple-element.14, f32[2,2048,640]{2,1,0:T(8,128)} %param.21, ...), kind=kLoop, calls=%fused_computation.44 | loop fusion | flops 49807360 | bytes 57671680 | tf_op jit(solution)/shard_map/convert_element_type | solution.py:30
  556.9 35.1 %fusion.15 = (bf16[2,640,2048]{2,1,0:T(8,128)(2,1)}, f32[2,640,2048]{2,1,0:T(8,128)}, f32[2,640,2048]{2,1,0:T(8,128)}, bf16[2,640,2048]{2,1,0:T(8,128)(2,1)}, f3...) fusion(bf16[2,640,2048]{2,1,0:T(8,128)(2,1)} %param.13, bf16[1,640,2048]{2,1,0:T(8,128)(2,1)S(1)} %copy-done.6, ...), kind=kLoop, calls=%fused_computation.36 | loop fusion | flops 99614720 | bytes 115343360 | tf_op jit(solution)/shard_map/convert_element_type | solution.py:30
  (44 shorter events, 0.1 us)
Async XLA Ops:
  7.2 527.7 %all-reduce.3.cloned.1.call-start = ((), (), s32[]{:S(2)}) async-start(), calls=%async_computation | async-start | bytes 31457280 | tf_op jit(solution)/shard_map/psum | solution.py:45
  10.2 45.0 %copy-start.1 = (bf16[1,2048,640]{1,2,0:T(8,128)(2,1)}, bf16[1,2048,640]{1,2,0:T(8,128)(2,1)S(1)}, u32[]{:S(2)}) copy-start(bf16[1,2048,640]{1,2,0:T(8,128)(2,1)S(1)} %copy.20) | copy-start | bytes 7864324
  10.8 27.6 %copy-start.9 = (f32[2048]{0:T(1024)}, f32[2048]{0:T(1024)S(1)}, u32[]{:S(2)}) copy-start(f32[2048]{0:T(1024)S(1)} %add_rsqrt_fusion) | copy-start | bytes 24580
  15.5 11.3 %copy-start.5 = (bf16[1,2048,640]{2,1,0:T(8,128)(2,1)S(1)}, bf16[1,2048,640]{2,1,0:T(8,128)(2,1)}, u32[]{:S(2)}) copy-start(bf16[1,2048,640]{2,1,0:T(8,128)(2,1)} %param.11) | copy-start | bytes 7864324
  64.4 1.5 copy-start.3
  64.4 1.5 copy-start.7
  78.1 55.4 %slice-start.2 = ((s8[5242880]{0:T(1024)(128)(4,1)}), s8[1048576]{0:T(1024)(128)(4,1)S(1)}, s32[]{:S(2)}) async-start(s8[5242880]{0:T(1024)(128)(4,1)} %bitcast.76), calls=%async_computation.3 | async-start | bytes 2097152
  103.2 30.2 %slice-start.3 = ((s8[5242880]{0:T(1024)(128)(4,1)}), s8[4194304]{0:T(1024)(128)(4,1)S(1)}, s32[]{:S(2)}) async-start(s8[5242880]{0:T(1024)(128)(4,1)} %bitcast.76), calls=%async_computation.4 | async-start | bytes 8388608
  120.2 36.7 %slice-start = ((s8[5242880]{0:T(1024)(128)(4,1)}), s8[4194304]{0:T(1024)(128)(4,1)S(1)}, s32[]{:S(2)}) async-start(s8[5242880]{0:T(1024)(128)(4,1)} %bitcast.74), calls=%async_computation.1 | async-start | bytes 8388608
  133.5 23.3 %slice-start.1 = ((s8[5242880]{0:T(1024)(128)(4,1)}), s8[1048576]{0:T(1024)(128)(4,1)S(1)}, s32[]{:S(2)}) async-start(s8[5242880]{0:T(1024)(128)(4,1)} %bitcast.74), calls=%async_computation.2 | async-start | bytes 2097152
  145.9 10.9 %copy-start.4 = (bf16[2048,640]{0,1:T(8,128)(2,1)S(1)}, bf16[2048,640]{0,1:T(8,128)(2,1)}, u32[]{:S(2)}) copy-start(bf16[2048,640]{0,1:T(8,128)(2,1)} %copy-done.3) | copy-start | bytes 7864324
  145.9 10.9 %copy-start.12 = (bf16[2048,640]{0,1:T(8,128)(2,1)S(1)}, bf16[2048,640]{0,1:T(8,128)(2,1)}, u32[]{:S(2)}) copy-start(bf16[2048,640]{0,1:T(8,128)(2,1)} %fusion.38) | copy-start | bytes 7864324
  156.9 8.5 %copy-start.8 = (f32[2048]{0:T(1024)S(1)}, f32[2048]{0:T(1024)}, u32[]{:S(2)}) copy-start(f32[2048]{0:T(1024)} %copy-done.7) | copy-start | bytes 24580
  156.9 8.5 %copy-start = (bf16[1,2048,640]{1,2,0:T(8,128)(2,1)S(1)}, bf16[1,2048,640]{1,2,0:T(8,128)(2,1)}, u32[]{:S(2)}) copy-start(bf16[1,2048,640]{1,2,0:T(8,128)(2,1)} %copy.21) | copy-start | bytes 7864324
  165.4 12.5 %slice-start.4 = ((s8[5242880]{0:T(1024)(128)(4,1)}), s8[1048576]{0:T(1024)(128)(4,1)S(1)}, s32[]{:S(2)}) async-start(s8[5242880]{0:T(1024)(128)(4,1)} %bitcast.78), calls=%async_computation.5 | async-start | bytes 2097152
  167.5 10.5 %slice-start.5 = ((s8[5242880]{0:T(1024)(128)(4,1)}), s8[4194304]{0:T(1024)(128)(4,1)S(1)}, s32[]{:S(2)}) async-start(s8[5242880]{0:T(1024)(128)(4,1)} %bitcast.78), calls=%async_computation.6 | async-start | bytes 8388608
  177.9 7.3 %copy-start.2 = (bf16[1,2048,640]{1,2,0:T(8,128)(2,1)S(1)}, bf16[1,2048,640]{1,2,0:T(8,128)(2,1)}, u32[]{:S(2)}) copy-start(bf16[1,2048,640]{1,2,0:T(8,128)(2,1)} %copy-done.1) | copy-start | bytes 7864324
  178.0 7.3 %copy-start.10 = (f32[2048]{0:T(1024)S(1)}, f32[2048]{0:T(1024)}, u32[]{:S(2)}) copy-start(f32[2048]{0:T(1024)} %copy-done.9) | copy-start | bytes 24580
  185.3 13.9 %copy-start.11 = (bf16[2048,2048]{1,0:T(8,128)(2,1)}, bf16[2048,2048]{1,0:T(8,128)(2,1)S(1)}, u32[]{:S(2)}) copy-start(bf16[2048,2048]{1,0:T(8,128)(2,1)S(1)} %convolution_convert_fusion) | copy-start | bytes 25165828
  534.9 22.1 %copy-start.6 = (bf16[1,640,2048]{2,1,0:T(8,128)(2,1)S(1)}, bf16[1,640,2048]{2,1,0:T(8,128)(2,1)}, u32[]{:S(2)}) copy-start(bf16[1,640,2048]{2,1,0:T(8,128)(2,1)} %get-tuple-element.9) | copy-start | bytes 7864324
Sparse Core Ops, SparseCore 0:
  218.4 316.4 all-reduce.2
where the time goes:
time: 608 us; the launch traced here: 599 us
  waiting for transfers between devices  317 us (52%)
  matrix products  199 us (33%)
  other arithmetic  59.8 us (10%)
  between operations  14.7 us (2%)
  local copies, waits for them, and re-layouts  9.26 us (2%)
    psum x1, waiting for transfers between devices, step(): summed[number] = [lax.psum(by_w[name], 'dp') for name in NAMES]  317 us
    dot_general x5, matrix products, layer(): gate = jnp.dot(a, w['w_gate'], preferred_element_type=jnp.float32)  75.1 us
    dot_general x5, matrix products, layer(): up = jnp.dot(a, w['w_up'], preferred_element_type=jnp.float32)  68.7 us
    convert_element_type x2, other arithmetic, adamw(): return ((w - 0.02 * step).astype(jnp.bfloat16), m, v)  57.1 us
    dot_general x5, matrix products, matmul(): jnp.dot(a, w, preferred_element_type=jnp.float32).astype(jnp.bfloat16)  55.1 us
  transfers between devices with their start and end apart: 1, of which 1 were waited for; matrix products, arithmetic and copies ran while one was open for 0% of the time, Pallas kernels for 0%

commit v1 on v0

v1 whole, which is shorter than its diff:
```python
import functools

import jax
import jax.numpy as jnp
from jax import lax
from jax.experimental import pallas as pl
from jax.experimental.pallas import tpu as pltpu
from jax.sharding import PartitionSpec as P

T, D, FF = 2048, 640, 2048
FS = 256
SLICES = FF // FS
CHUNKS = 2 * SLICES * 3
SLOTS = 8
LAST = 12
HALF = D // 2
ROWS = 512
F32, BF16 = jnp.float32, jnp.bfloat16
MESH = pl.DeviceIdType.MESH


def normed(h):
    wide = h.astype(F32)
    scale = lax.rsqrt(jnp.mean(wide**2, -1, keepdims=True) + 1e-6)
    return (wide * scale).astype(BF16)


def matmul(a, w):
    return jnp.dot(a, w, preferred_element_type=F32).astype(BF16)


def adamw(w, m, v, g):
    m = 0.9 * m + 0.1 * g
    v = 0.95 * v + 0.05 * g * g
    step = m * lax.rsqrt(v + 1e-8) + 0.1 * w
    return (w - 0.02 * step).astype(BF16), m, v


def dot_t(a, b):
    return lax.dot_general(a, b, (((1,), (1,)), ((), ())), preferred_element_type=F32)


def kernel(
    a0_in, a1_in, h_in, dy_in, wg_in, wu_in, wd_in, out,
    a, at, dz, dzt, h, da, wgu, wd, act, dgu,
    g, xb, ab, bb, sb, tot,
    load_sem, w_sem, sx, rx, ss, ra, rb, sc, rc, sy, ry, so,
):
    at_dp = lax.axis_index("dp")
    c = lax.rem(at_dp, 2)
    z = lax.div(at_dp, 2)
    is_end = (z == 0) | (z == 3)
    is_mid = (z == 1) | (z == 2)
    partner = z * 2 + 1 - c
    inner = jnp.where(z == 0, 1, 2) * 2 + c
    outer = jnp.where(z == 1, 0, 3) * 2 + c
    across = (3 - z) * 2 + c
    own = pl.ds(pl.multiple_of(c * HALF, HALF), HALF)
    other = pl.ds(pl.multiple_of((1 - c) * HALF, HALF), HALF)

    def load(src, dst, i):
        return pltpu.make_async_copy(src, dst, load_sem.at[i])

    loads = [
        load(a1_in, a.at[1], 0),
        load(dy_in, dz, 1),
        load(a0_in, a.at[0], 2),
        load(h_in, h, 3),
    ]

    def weights(s):
        slot = lax.rem(s, 2)
        layer = 1 - lax.div(s, SLICES)
        cols = pl.ds(pl.multiple_of(lax.rem(s, SLICES) * FS, FS), FS)
        return [
            pltpu.make_async_copy(wg_in.at[layer, :, cols], wgu.at[slot, :, pl.ds(0, FS)], w_sem.at[slot, 0]),
            pltpu.make_async_copy(wu_in.at[layer, :, cols], wgu.at[slot, :, pl.ds(FS, FS)], w_sem.at[slot, 1]),
            pltpu.make_async_copy(wd_in.at[layer, cols, :], wd.at[slot], w_sem.at[slot, 2]),
        ]

    loads[0].start()
    for copy in weights(0):
        copy.start()
    for one in loads[1:]:
        one.start()

    barrier = pltpu.get_barrier_semaphore()

    def greet(device):
        pl.semaphore_signal(barrier, inc=1, device_id={"dp": device}, device_id_type=MESH)

    greet(partner)

    @pl.when(is_end)
    def _():
        greet(inner)
        pl.semaphore_wait(barrier, 2)

    @pl.when(is_mid)
    def _():
        greet(outer)
        greet(across)
        pl.semaphore_wait(barrier, 3)

    def remote(src, dst, send, recv, device):
        return pltpu.make_async_remote_copy(
            src_ref=src, dst_ref=dst, send_sem=send, recv_sem=recv, device_id={"dp": device}, device_id_type=MESH
        )

    def copy_x(i):
        return remote(g.at[i, other], xb.at[i], sx.at[i], rx.at[i], partner)

    def copy_a(i):
        return remote(sb.at[i], ab.at[i], ss.at[i], ra.at[i], inner)

    def copy_b(i):
        return remote(sb.at[i], bb.at[i], ss.at[i], rb.at[i], across)

    def copy_c(i):
        return remote(tot.at[i, own], tot.at[i, own], sc.at[i], rc.at[i], outer)

    def copy_y(i):
        return remote(tot.at[i, own], tot.at[i, own], sy.at[i], ry.at[i], partner)

    def copy_out(j):
        i = lax.rem(j, LAST)
        s = lax.div(j, 3)
        row = (1 - lax.div(s, SLICES)) * 3 + lax.rem(j, 3)
        cols = pl.ds(pl.multiple_of(lax.rem(s, SLICES) * FS, FS), FS)
        return pltpu.make_async_copy(tot.at[i], out.at[row, :, cols], so.at[i])

    def stage(j, only=None):
        cond = (j >= 0) & (j < CHUNKS)
        if only is not None:
            cond = cond & only
        return pl.when(cond)

    def tick(k):
        @stage(k)
        def _():
            copy_x(lax.rem(k, SLOTS)).start()

        j1 = k - 1

        @stage(j1)
        def _():
            i = lax.rem(j1, SLOTS)
            copy_x(i).wait_recv()
            copy_x(i).wait_send()

            @pl.when(is_end)
            def _():
                sb[i] = (g[i, own].astype(F32) + xb[i].astype(F32)).astype(BF16)
                copy_a(i).start()

        j2 = k - 3

        @stage(j2, is_mid)
        def _():
            i = lax.rem(j2, SLOTS)
            copy_a(i).wait_recv()
            sb[i] = (g[i, own].astype(F32) + xb[i].astype(F32) + ab[i].astype(F32)).astype(BF16)
            copy_b(i).start()

        j3 = k - 5

        @stage(j3, is_mid)
        def _():
            i, t = lax.rem(j3, SLOTS), lax.rem(j3, LAST)
            copy_b(i).wait_recv()
            tot[t, own] = (sb[i].astype(F32) + bb[i].astype(F32)).astype(BF16)
            copy_c(t).start()
            copy_y(t).start()
            copy_b(i).wait_send()

        j4 = k - 7

        @stage(j4, is_end)
        def _():
            i, t = lax.rem(j4, SLOTS), lax.rem(j4, LAST)
            copy_c(t).wait_recv()
            copy_y(t).start()
            copy_a(i).wait_send()

        j5 = k - 8

        @stage(j5)
        def _():
            t = lax.rem(j5, LAST)
            copy_y(t).wait_recv()
            copy_y(t).wait_send()

            @pl.when(is_mid)
            def _():
                copy_c(t).wait_send()

            copy_out(j5).start()

        j6 = k - 9

        @stage(j6)
        def _():
            copy_out(j6).wait()

    def transpose(src, dst):
        for r in range(T // ROWS):
            dst[:, r * ROWS : (r + 1) * ROWS] = src[r * ROWS : (r + 1) * ROWS, :].T

    def slice_(s, _):
        slot = lax.rem(s, 2)
        layer = 1 - lax.div(s, SLICES)

        @pl.when(s == 0)
        def _():
            loads[0].wait()
            loads[1].wait()

        for copy in weights(s):
            copy.wait()

        @pl.when(s + 1 < 2 * SLICES)
        def _():
            for copy in weights(s + 1):
                copy.start()

        @pl.when(s == SLICES)
        def _():
            loads[2].wait()
            loads[3].wait()

            def block(r, _):
                rows = pl.ds(pl.multiple_of(r * ROWS, ROWS), ROWS)
                wide = h[rows].astype(F32)
                by_a = da[rows].astype(BF16).astype(F32)
                scale = lax.rsqrt(jnp.mean(wide * wide, -1, keepdims=True) + 1e-6)
                back = jnp.mean(by_a * wide, -1, keepdims=True) * (scale * scale * scale)
                by_h = (by_a * scale - wide * back).astype(BF16)
                dz[rows] = (dz[rows].astype(F32) + by_h.astype(F32)).astype(BF16)
                return ()

            lax.fori_loop(0, T // ROWS, block, ())

        def block(r, _):
            rows = pl.ds(pl.multiple_of(r * ROWS, ROWS), ROWS)
            both = jnp.dot(a[layer, rows], wgu[slot], preferred_element_type=F32)
            gate, up = both[:, :FS], both[:, FS:]
            by_act = dot_t(dz[rows], wd[slot]).astype(BF16).astype(F32)
            sig = jax.nn.sigmoid(gate)
            silu = gate * sig
            act[rows] = (silu * up).astype(BF16)
            by_gate = (by_act * up * (sig * (1 + gate * (1 - sig)))).astype(BF16)
            by_up = (by_act * silu).astype(BF16)
            dgu[rows, :FS] = by_gate
            dgu[rows, FS:] = by_up

            @pl.when(s < SLICES)
            def _():
                part = dot_t(dgu[rows], wgu[slot])

                @pl.when(s == 0)
                def _():
                    da[rows] = part

                @pl.when(s > 0)
                def _():
                    da[rows] += part

            return ()

        half = T // ROWS // 2
        lax.fori_loop(0, half, block, ())
        tick(3 * s - 1)
        lax.fori_loop(half, 2 * half, block, ())

        @pl.when(lax.rem(s, SLICES) == 0)
        def _():
            transpose(dz, dzt)
            transpose(a.at[layer], at)

        g[lax.rem(3 * s, SLOTS)] = jnp.dot(dzt[...], act[...], preferred_element_type=F32).astype(BF16)
        tick(3 * s)
        both = jnp.dot(at[...], dgu[...], preferred_element_type=F32).astype(BF16)
        g[lax.rem(3 * s + 1, SLOTS)] = both[:, :FS]
        g[lax.rem(3 * s + 2, SLOTS)] = both[:, FS:]
        tick(3 * s + 1)
        return ()

    lax.fori_loop(0, 2 * SLICES, slice_, ())

    def drain(k, _):
        tick(k)
        return ()

    lax.fori_loop(CHUNKS - 1, CHUNKS + 10, drain, ())


def gradients(a0, a1, h1, dy, wg, wu, wd):
    dma = lambda *n: pltpu.SemaphoreType.DMA(n)
    any_ = pl.BlockSpec(memory_space=pl.ANY)
    return pl.pallas_call(
        kernel,
        out_shape=jax.ShapeDtypeStruct((6, D, FF), BF16),
        in_specs=[any_] * 7,
        out_specs=any_,
        scratch_shapes=[
            pltpu.VMEM((2, T, D), BF16),
            pltpu.VMEM((D, T), BF16),
            pltpu.VMEM((T, D), BF16),
            pltpu.VMEM((D, T), BF16),
            pltpu.VMEM((T, D), BF16),
            pltpu.VMEM((T, D), F32),
            pltpu.VMEM((2, D, 2 * FS), BF16),
            pltpu.VMEM((2, FS, D), BF16),
            pltpu.VMEM((T, FS), BF16),
            pltpu.VMEM((T, 2 * FS), BF16),
            pltpu.VMEM((SLOTS, D, FS), BF16),
            pltpu.VMEM((SLOTS, HALF, FS), BF16),
            pltpu.VMEM((SLOTS, HALF, FS), BF16),
            pltpu.VMEM((SLOTS, HALF, FS), BF16),
            pltpu.VMEM((SLOTS, HALF, FS), BF16),
            pltpu.VMEM((LAST, D, FS), BF16),
            dma(4),
            dma(2, 3),
        ]
        + [dma(SLOTS)] * 5
        + [dma(LAST)] * 5,
        compiler_params=pltpu.CompilerParams(collective_id=0, has_side_effects=True, vmem_limit_bytes=60 * 2**20),
        cost_estimate=pl.CostEstimate(flops=90 * 10**9, bytes_accessed=60 * 2**20, transcendentals=0),
        name="backward_sum",
    )(a0, a1, h1, dy, wg, wu, wd)


def solution(mesh):
    def step(x, dy, *arrays):
        weights, m, v = (arrays[i : i + 3] for i in (0, 3, 6))
        wg, wu, wd = weights
        h0 = x[0]
        a0 = normed(h0)
        gate = jnp.dot(a0, wg[0], preferred_element_type=F32)
        up = jnp.dot(a0, wu[0], preferred_element_type=F32)
        h1 = h0 + matmul((jax.nn.silu(gate) * up).astype(BF16), wd[0])
        a1 = normed(h1)
        summed = gradients(a0, a1, h1, dy[0], wg, wu, wd).reshape(2, 3, D, FF)
        grads = [summed[:, 1], summed[:, 2], jnp.swapaxes(summed[:, 0], 1, 2)]
        new = [adamw(w.astype(F32), m, v, g.astype(F32)) for w, m, v, g in zip(weights, m, v, grads, strict=True)]
        return tuple(one[which] for which in range(3) for one in new)

    return jax.shard_map(
        step,
        mesh=mesh,
        in_specs=(P(("rep", "dp"), None, None),) * 2 + (P(None, None, None),) * 9,
        out_specs=(P("rep", None, None),) * 9,
        check_vma=False,
    )
```

time: 608 us -> 318 us (0.52); the launches traced: 599 us -> 318 us
  waiting for transfers between devices: 317 us -> 0 us
  Pallas kernels: 0 us -> 204 us
  matrix products: 199 us -> 32 us
  between operations: 14.7 us -> 0.67 us
  other arithmetic: 59.8 us -> 68.1 us
    psum x1 -> x0, waiting for transfers between devices: 317 us -> none  [step(): summed[number] = [lax.psum(by_w[name], 'dp') for name in NAMES]]
    pallas_call x0 -> x1, Pallas kernels: none -> 204 us  [gradients(): pl.pallas_call(kernel, out_shape=jax.ShapeDtypeStruct((6, D, FF), BF16),...]
    dot_general x15 -> x2, matrix products: 199 us -> 32 us  [the longest x1 19.5 us: matmul(): return jnp.dot(a, w, preferred_element_type=F32).astype(BF16)]
    convert_element_type x2 -> x3, other arithmetic: 57.1 us -> 65.8 us  [the longest x2 61.6 us: adamw(): return ((w - 0.02 * step).astype(BF16), m, v)]
  transfers between devices with their start and end apart: 1 -> 0, of which waited for: 1 -> 0; matrix products, arithmetic and copies ran while one was open for 0% -> 0% of each run, Pallas kernels for 0% -> 0%
where the time goes in v1:
time: 318 us
  Pallas kernels  204 us (64%)
  other arithmetic  68.1 us (21%)
  matrix products  32 us (10%)
  local copies, waits for them, and re-layouts  13.6 us (4%)
    pallas_call x1, Pallas kernels, gradients(): pl.pallas_call(kernel, out_shape=jax.ShapeDtypeStruct((6, D, FF), BF16),...  204 us
    convert_element_type x2, other arithmetic, adamw(): return ((w - 0.02 * step).astype(BF16), m, v)  61.6 us
    dot_general x1, matrix products, matmul(): return jnp.dot(a, w, preferred_element_type=F32).astype(BF16)  19.5 us
    dot_general x1, matrix products, step(): gate = jnp.dot(a0, wg[0], preferred_element_type=F32)  12.5 us
    unnamed x3, local copies, waits for them, and re-layouts  7.9 us

profile of v1, /device:TPU:0, one launch (start us, length us, event | category | flops | bytes accessed | tf_op | source)
XLA Modules:
  0.0 317.9 jit_solution(8314101982041646288)
XLA Ops:
  0.6 2.3 fusion.16
  3.0 0.0 copy-start
  3.0 12.5 %fusion.25 = f32[2048,2048]{1,0:T(8,128)} fusion(bf16[2,640,2048]{2,1,0:T(8,128)(2,1)} %wg_in.1, bf16[1,2048,640]{2,1,0:T(8,128)(2,1)} %param.11, f32[2048]{0:T(1024)S(1)} %add_rsqrt_fusion.1), kind=kOutput, calls=%fused_computation.46 | convolution fusion | flops 5372641280 | bytes 22028288 | tf_op jit(solution)/shard_map/dot_general | solution.py:339
  15.5 0.0 copy-done
  15.5 19.5 %fusion.18 = (f32[2048]{0:T(1024)S(1)}, bf16[2048,640]{1,0:T(8,128)(2,1)}) fusion(bf16[2,2048,640]{2,1,0:T(8,128)(2,1)} %wd_in.1, f32[2048,2048]{1,0:T(8,128)} %fusion.25, bf16[2,640,2048]{2,1,0:T(8,128)(2,1)} %wu_in.1, bf16[1,2048,640]{2,1,0:T(8,128)(2,1)S(1)} %copy-done, f32[2048]{0:T(1024)S(1)} %add_rsqrt_fusion.1), kind=kOutput, calls=%fused_computation.37 | convolution fusion | flops 10776999936 | bytes 29900800 | tf_op jit(solution)/shard_map/dot_general | solution.py:29
  35.0 4.2 %fusion.17 = (bf16[2048,640]{1,0:T(8,128)(2,1)}, bf16[2048,640]{1,0:T(8,128)(2,1)}) fusion(bf16[1,2048,640]{2,1,0:T(8,128)(2,1)S(1)} %copy-done, f32[2048]{0:T(1024)S(1)} %add_rsqrt_fusion.1, f32[2048]{0:T(1024)S(1)} %add_rsqrt_fusion, bf16[2048,640]{1,0:T(8,128)(2,1)} %get-tuple-element.22.h_in), kind=kLoop, calls=%fused_computation.36 | loop fusion | flops 7864320 | bytes 10502144 | tf_op jit(solution)/shard_map/convert_element_type | solution.py:25
  39.2 203.5 %backward_sum.1 = bf16[6,640,2048]{2,1,0:T(8,128)(2,1)} custom-call(bf16[2048,640]{1,0:T(8,128)(2,1)} %get-tuple-element.23.a0_in, bf16[2048,640]{1,0:T(8,128)(2,1)} %get-tuple-element.24.a1_in, bf16[2048,640]{1,0:T(8,128)(2,1)} %get-tuple-element.22.h_in, bf16[2048,640]{1,0:T(8,128)(2,1)} %bitcast.72, bf16[2,640,2048]{2,1,0:T(8,128)(2,1)} %wg_in.1, ...), custom_call_target="tpu_custom_call" | custom-call | flops 89999998976 | bytes 62914560 | tf_op jit(solution)/shard_map/backward_sum/pallas_call | solution.py:300
  242.7 39.9 %fusion.5 = (bf16[2,640,2048]{2,1,0:T(8,128)(2,1)}, f32[2,640,2048]{2,1,0:T(8,128)}, f32[2,640,2048]{2,1,0:T(8,128)}, bf16[2,640,2048]{2,1,0:T(8,128)(2,1)}, f32...) fusion(bf16[2,640,2048]{2,1,0:T(8,128)(2,1)} %wu_in.1, bf16[2,3,640,2048]{3,2,1,0:T(8,128)(2,1)} %bitcast.70, ...), kind=kLoop, calls=%fused_computation.19 | loop fusion | flops 83886080 | bytes 115343360 | tf_op jit(solution)/shard_map/convert_element_type | solution.py:36
  282.7 5.7 %slice.26 = bf16[2,1,640,2048]{3,2,1,0:T(8,128)(2,1)} slice(bf16[2,3,640,2048]{3,2,1,0:T(8,128)(2,1)} %bitcast.71), slice={[0:2], [0:1], [0:640], [0:2048]} | slice | bytes 10485760 | tf_op jit(solution)/shard_map/slice | solution.py:344
  288.4 7.9 %copy.27 = bf16[2,1,640,2048]{2,3,0,1:T(8,128)(2,1)} copy(bf16[2,1,640,2048]{3,2,1,0:T(8,128)(2,1)} %slice.26) | data formatting | bytes 10485760
  296.2 21.7 %fusion.8 = (bf16[2,2048,640]{2,1,0:T(8,128)(2,1)}, f32[2,2048,640]{2,1,0:T(8,128)}, f32[2,2048,640]{2,1,0:T(8,128)}) fusion(bf16[2,2048,640]{2,1,0:T(8,128)(2,1)} %wd_in.1, bf16[2,1,640,2048]{2,3,0,1:T(8,128)(2,1)} %copy.27, f32[2,2048,640]{2,1,0:T(8,128)} %param.21, f32[2,2048,640]{2,1,0:T(8,128)} %param.18), kind=kLoop, calls=%fused_computation.22 | loop fusion | flops 41943040 | bytes 57671680 | tf_op jit(solution)/shard_map/convert_element_type | solution.py:36
  (2 shorter events, 0.0 us)
Async XLA Ops:
  3.0 12.5 %copy-start = (bf16[1,2048,640]{2,1,0:T(8,128)(2,1)S(1)}, bf16[1,2048,640]{2,1,0:T(8,128)(2,1)}, u32[]{:S(2)}) copy-start(bf16[1,2048,640]{2,1,0:T(8,128)(2,1)} %param.11) | copy-start | bytes 7864324

commit v2 on v0

v2 whole, which is shorter than its diff:
```python
import jax
import jax.numpy as jnp
from jax import lax
from jax.experimental import pallas as pl
from jax.experimental.pallas import tpu as pltpu
from jax.sharding import PartitionSpec as P

T, D, FF = 2048, 640, 2048
FS = 256
SLICES = FF // FS
CHUNKS = 2 * SLICES * 3
PARTS = 2
UNITS = CHUNKS * PARTS
SLOTS = 8
MESSAGES = SLOTS * PARTS
LAST = 12
HALF = D // 2
PIECE = HALF // PARTS
ROWS = 512
FROWS = 512
NROWS = 256
F32, BF16 = jnp.float32, jnp.bfloat16
MESH = pl.DeviceIdType.MESH


def normed(h):
    wide = h.astype(F32)
    scale = lax.rsqrt(jnp.mean(wide**2, -1, keepdims=True) + 1e-6)
    return (wide * scale).astype(BF16)


def adamw(w, m, v, g):
    m = 0.9 * m + 0.1 * g
    v = 0.95 * v + 0.05 * g * g
    step = m * lax.rsqrt(v + 1e-8) + 0.1 * w
    return (w - 0.02 * step).astype(BF16), m, v


AFTER = (2, 5, 8, 11, 13, 14)


def dot_t(a, b):
    return lax.dot_general(a, b, (((1,), (1,)), ((), ())), preferred_element_type=F32)


def kernel(
    x_in, dy_in, wg_in, wu_in, wd_in, out,
    a, at, dz, dzt, h, da, wgu, wd, act, dgu,
    g, xb, ab, bb, sb, tot,
    load_sem, w_sem, sx, rx, ss, ra, rb, sc, rc, sy, ry, so,
):
    at_dp = lax.axis_index("dp")
    c = lax.rem(at_dp, 2)
    z = lax.div(at_dp, 2)
    is_end = (z == 0) | (z == 3)
    is_mid = (z == 1) | (z == 2)
    partner = z * 2 + 1 - c
    inner = jnp.where(z == 0, 1, 2) * 2 + c
    outer = jnp.where(z == 1, 0, 3) * 2 + c
    across = (3 - z) * 2 + c
    def piece(u, core):
        return pl.ds(pl.multiple_of(core * HALF + lax.rem(u, PARTS) * PIECE, PIECE), PIECE)

    def load(src, dst, i):
        return pltpu.make_async_copy(src, dst, load_sem.at[i])

    loads = [load(x_in, h, 0), load(dy_in, dz, 1)]

    def weights(s):
        slot = lax.rem(s + SLICES, 2)
        layer = jnp.where((s >= 0) & (s < SLICES), 1, 0)
        cols = pl.ds(pl.multiple_of(lax.rem(s + SLICES, SLICES) * FS, FS), FS)
        return [
            pltpu.make_async_copy(wg_in.at[layer, :, cols], wgu.at[slot, :, pl.ds(0, FS)], w_sem.at[slot, 0]),
            pltpu.make_async_copy(wu_in.at[layer, :, cols], wgu.at[slot, :, pl.ds(FS, FS)], w_sem.at[slot, 1]),
            pltpu.make_async_copy(wd_in.at[layer, cols, :], wd.at[slot], w_sem.at[slot, 2]),
        ]

    loads[0].start()
    for copy in weights(-SLICES):
        copy.start()
    loads[1].start()

    barrier = pltpu.get_barrier_semaphore()

    def greet(device):
        pl.semaphore_signal(barrier, inc=1, device_id={"dp": device}, device_id_type=MESH)

    greet(partner)

    @pl.when(is_end)
    def _():
        greet(inner)
        pl.semaphore_wait(barrier, 2)

    @pl.when(is_mid)
    def _():
        greet(outer)
        greet(across)
        pl.semaphore_wait(barrier, 3)

    def remote(src, dst, send, recv, device):
        return pltpu.make_async_remote_copy(
            src_ref=src, dst_ref=dst, send_sem=send, recv_sem=recv, device_id={"dp": device}, device_id_type=MESH
        )

    def chunk(u):
        return lax.rem(lax.div(u, PARTS), SLOTS)

    def sums(u):
        return tot.at[lax.rem(lax.div(u, PARTS), LAST), piece(u, c)]

    def copy_x(u):
        i = lax.rem(u, MESSAGES)
        return remote(g.at[chunk(u), piece(u, 1 - c)], xb.at[i], sx.at[i], rx.at[i], partner)

    def copy_a(u):
        i = lax.rem(u, MESSAGES)
        return remote(sb.at[i], ab.at[i], ss.at[i], ra.at[i], inner)

    def copy_b(u):
        i = lax.rem(u, MESSAGES)
        return remote(sb.at[i], bb.at[i], ss.at[i], rb.at[i], across)

    def copy_c(u):
        i = lax.rem(u, LAST * PARTS)
        return remote(sums(u), sums(u), sc.at[i], rc.at[i], outer)

    def copy_y(u):
        i = lax.rem(u, LAST * PARTS)
        return remote(sums(u), sums(u), sy.at[i], ry.at[i], partner)

    def copy_out(u):
        k = lax.div(u, PARTS)
        i = lax.rem(k, LAST)
        s = lax.div(k, 3)
        row = (1 - lax.div(s, SLICES)) * 3 + lax.rem(k, 3)
        cols = pl.ds(pl.multiple_of(lax.rem(s, SLICES) * FS, FS), FS)
        return pltpu.make_async_copy(tot.at[i], out.at[row, :, cols], so.at[i])

    def stage(u, only=None):
        cond = (u >= 0) & (u < UNITS)
        if only is not None:
            cond = cond & only
        return pl.when(cond)

    def tick(u):
        @stage(u)
        def _():
            copy_x(u).start()

        u1 = u - AFTER[0]

        @stage(u1)
        def _():
            i = lax.rem(u1, MESSAGES)
            copy_x(u1).wait_recv()
            copy_x(u1).wait_send()

            @pl.when(is_end)
            def _():
                sb[i] = (g[chunk(u1), piece(u1, c)].astype(F32) + xb[i].astype(F32)).astype(BF16)
                copy_a(u1).start()

        u2 = u - AFTER[1]

        @stage(u2, is_mid)
        def _():
            i = lax.rem(u2, MESSAGES)
            copy_a(u2).wait_recv()
            sb[i] = (g[chunk(u2), piece(u2, c)].astype(F32) + xb[i].astype(F32) + ab[i].astype(F32)).astype(BF16)
            copy_b(u2).start()

        u3 = u - AFTER[2]

        @stage(u3, is_mid)
        def _():
            i = lax.rem(u3, MESSAGES)
            copy_b(u3).wait_recv()
            tot[lax.rem(lax.div(u3, PARTS), LAST), piece(u3, c)] = (sb[i].astype(F32) + bb[i].astype(F32)).astype(BF16)
            copy_c(u3).start()
            copy_y(u3).start()
            copy_b(u3).wait_send()

        u4 = u - AFTER[3]

        @stage(u4, is_end)
        def _():
            copy_c(u4).wait_recv()
            copy_y(u4).start()
            copy_a(u4).wait_send()

        u5 = u - AFTER[4]

        @stage(u5)
        def _():
            copy_y(u5).wait_recv()
            copy_y(u5).wait_send()

            @pl.when(is_mid)
            def _():
                copy_c(u5).wait_send()

            @pl.when(lax.rem(u5, PARTS) == PARTS - 1)
            def _():
                copy_out(u5).start()

        u6 = u - AFTER[5]

        @stage(u6, lax.rem(u6, PARTS) == PARTS - 1)
        def _():
            copy_out(u6).wait()

    def take_weights(s):
        for copy in weights(s):
            copy.wait()

        @pl.when(s + 1 < 2 * SLICES)
        def _():
            for copy in weights(s + 1):
                copy.start()

    def block_rows(r):
        return pl.ds(pl.multiple_of(r * ROWS, ROWS), ROWS)

    def norm_rows(r):
        return pl.ds(pl.multiple_of(r * NROWS, NROWS), NROWS)

    def each_norm(body):
        lax.fori_loop(0, T // NROWS, body, ())

    def each_block(body):
        lax.fori_loop(0, T // ROWS, body, ())

    loads[0].wait()

    def first_norm(r, _):
        rows = norm_rows(r)
        inputs = normed(h[rows])
        a[0, rows] = inputs
        at[0, :, rows] = inputs.T
        da[rows] = jnp.zeros((NROWS, D), F32)
        return ()

    each_norm(first_norm)
    loads[1].wait()

    def forward(f, _):
        slot = lax.rem(f, 2)
        take_weights(f - SLICES)
        turn = pl.ds(pl.multiple_of(f * FS, FS), FS)
        dzt[:, turn] = dz[turn].T
        for r in range(T // FROWS):
            rows = pl.ds(r * FROWS, FROWS)
            both = jnp.dot(a[0, rows], wgu[slot], preferred_element_type=F32)
            gate, up = both[:, :FS], both[:, FS:]
            hidden = (gate * jax.nn.sigmoid(gate) * up).astype(BF16)
            da[rows] += jnp.dot(hidden, wd[slot], preferred_element_type=F32)
        return ()

    lax.fori_loop(0, SLICES, forward, ())

    def second_norm(r, _):
        rows = norm_rows(r)
        states = (h[rows].astype(F32) + da[rows].astype(BF16).astype(F32)).astype(BF16)
        h[rows] = states
        inputs = normed(states)
        a[1, rows] = inputs
        at[1, :, rows] = inputs.T
        da[rows] = jnp.zeros((NROWS, D), F32)
        return ()

    each_norm(second_norm)

    def backward(s, layer):
        slot = lax.rem(s, 2)
        take_weights(s)

        def block(r, _):
            rows = block_rows(r)
            both = jnp.dot(a[layer, rows], wgu[slot], preferred_element_type=F32)
            gate, up = both[:, :FS], both[:, FS:]
            by_act = dot_t(dz[rows], wd[slot]).astype(BF16).astype(F32)
            sig = jax.nn.sigmoid(gate)
            silu = gate * sig
            act[rows] = (silu * up).astype(BF16)
            dgu[rows, :FS] = (by_act * up * (sig * (1 + gate * (1 - sig)))).astype(BF16)
            dgu[rows, FS:] = (by_act * silu).astype(BF16)
            if layer == 1:
                da[rows] += dot_t(dgu[rows], wgu[slot])
            tick(6 * s - 4 + r)
            return ()

        each_block(block)
        g[lax.rem(3 * s, SLOTS)] = jnp.dot(dzt[...], act[...], preferred_element_type=F32).astype(BF16)
        tick(6 * s)
        both = jnp.dot(at[layer], dgu[...], preferred_element_type=F32).astype(BF16)
        g[lax.rem(3 * s + 1, SLOTS)] = both[:, :FS]
        g[lax.rem(3 * s + 2, SLOTS)] = both[:, FS:]
        tick(6 * s + 1)

    def last_layer(s, _):
        backward(s, 1)
        return ()

    def first_layer(s, _):
        backward(s, 0)
        return ()

    lax.fori_loop(0, SLICES, last_layer, ())

    def between(r, _):
        rows = norm_rows(r)
        wide = h[rows].astype(F32)
        by_a = da[rows].astype(BF16).astype(F32)
        scale = lax.rsqrt(jnp.mean(wide * wide, -1, keepdims=True) + 1e-6)
        back = jnp.mean(by_a * wide, -1, keepdims=True) * (scale * scale * scale)
        by_h = (by_a * scale - wide * back).astype(BF16)
        total = (dz[rows].astype(F32) + by_h.astype(F32)).astype(BF16)
        dz[rows] = total
        dzt[:, rows] = total.T
        return ()

    each_norm(between)
    lax.fori_loop(SLICES, 2 * SLICES, first_layer, ())

    def drain(u, _):
        tick(u)
        return ()

    lax.fori_loop(UNITS - 4, UNITS + AFTER[-1] + 1, drain, ())


def gradients(x, dy, wg, wu, wd):
    dma = lambda *n: pltpu.SemaphoreType.DMA(n)
    any_ = pl.BlockSpec(memory_space=pl.ANY)
    return pl.pallas_call(
        kernel,
        out_shape=jax.ShapeDtypeStruct((6, D, FF), BF16),
        in_specs=[any_] * 5,
        out_specs=any_,
        scratch_shapes=[
            pltpu.VMEM((2, T, D), BF16),
            pltpu.VMEM((2, D, T), BF16),
            pltpu.VMEM((T, D), BF16),
            pltpu.VMEM((D, T), BF16),
            pltpu.VMEM((T, D), BF16),
            pltpu.VMEM((T, D), F32),
            pltpu.VMEM((2, D, 2 * FS), BF16),
            pltpu.VMEM((2, FS, D), BF16),
            pltpu.VMEM((T, FS), BF16),
            pltpu.VMEM((T, 2 * FS), BF16),
            pltpu.VMEM((SLOTS, D, FS), BF16),
            pltpu.VMEM((MESSAGES, PIECE, FS), BF16),
            pltpu.VMEM((MESSAGES, PIECE, FS), BF16),
            pltpu.VMEM((MESSAGES, PIECE, FS), BF16),
            pltpu.VMEM((MESSAGES, PIECE, FS), BF16),
            pltpu.VMEM((LAST, D, FS), BF16),
            dma(2),
            dma(2, 3),
        ]
        + [dma(MESSAGES)] * 5
        + [dma(LAST * PARTS)] * 4
        + [dma(LAST)],
        compiler_params=pltpu.CompilerParams(collective_id=0, has_side_effects=True, vmem_limit_bytes=63 * 2**20),
        cost_estimate=pl.CostEstimate(flops=95 * 10**9, bytes_accessed=60 * 2**20, transcendentals=0),
        name="backward_sum",
    )(x, dy, wg, wu, wd)


def adamw_kernel(*refs):
    g_refs, w_refs, m_refs, v_refs, wo_refs, mo_refs, vo_refs = (refs[i : i + 3] for i in range(0, 21, 3))
    turned = refs[21]
    turned[...] = g_refs[2][0].T
    for n in range(3):
        count, rows = (5, 16) if n < 2 else (8, 32)

        def part(r, _, n=n, rows=rows):
            at = pl.ds(pl.multiple_of(r * rows, rows), rows)
            g = (g_refs[n][0, at] if n < 2 else turned[at]).astype(F32)
            w, m, v = adamw(w_refs[n][0, at].astype(F32), m_refs[n][0, at], v_refs[n][0, at], g)
            wo_refs[n][0, at] = w
            mo_refs[n][0, at] = m
            vo_refs[n][0, at] = v
            return ()

        lax.fori_loop(0, count, part, (), unroll=True)


def optimizer(summed, weights, m, v):
    steps = 8
    wide = pl.BlockSpec((1, D // steps, FF), lambda l, i: (l, i, 0))
    tall = pl.BlockSpec((1, FF // steps, D), lambda l, i: (l, i, 0))
    each = [wide, wide, tall]
    g_specs = [
        pl.BlockSpec((1, D // steps, FF), lambda l, i: (3 * l + 1, i, 0)),
        pl.BlockSpec((1, D // steps, FF), lambda l, i: (3 * l + 2, i, 0)),
        pl.BlockSpec((1, D, FF // steps), lambda l, i: (3 * l, 0, i)),
    ]
    shapes = [jax.ShapeDtypeStruct(one.shape, one.dtype) for one in (*weights, *m, *v)]
    return pl.pallas_call(
        adamw_kernel,
        grid=(2, steps),
        out_shape=shapes,
        in_specs=g_specs + each * 3,
        out_specs=each * 3,
        scratch_shapes=[pltpu.VMEM((FF // steps, D), BF16)],
        compiler_params=pltpu.CompilerParams(vmem_limit_bytes=63 * 2**20),
        cost_estimate=pl.CostEstimate(flops=120 * 10**6, bytes_accessed=173 * 10**6, transcendentals=8 * 10**6),
        name="adamw",
    )(summed, summed, summed, *weights, *m, *v)


def solution(mesh):
    def step(x, dy, *arrays):
        weights, m, v = (arrays[i : i + 3] for i in (0, 3, 6))
        summed = gradients(x[0], dy[0], *weights)
        return tuple(optimizer(summed, weights, m, v))

    return jax.shard_map(
        step,
        mesh=mesh,
        in_specs=(P(("rep", "dp"), None, None),) * 2 + (P(None, None, None),) * 9,
        out_specs=(P("rep", None, None),) * 9,
        check_vma=False,
    )
```

time: 608 us -> 283 us (0.47); the launches traced: 599 us -> 283 us
  waiting for transfers between devices: 317 us -> 0 us
  Pallas kernels: 0 us -> 282 us
  matrix products: 199 us -> 0 us
  other arithmetic: 59.8 us -> 0 us
  between operations: 14.7 us -> 0.65 us
  local copies, waits for them, and re-layouts: 9.26 us -> 0 us
    psum x1 -> x0, waiting for transfers between devices: 317 us -> none  [step(): summed[number] = [lax.psum(by_w[name], 'dp') for name in NAMES]]
    pallas_call x0 -> x2, Pallas kernels: none -> 282 us  [the longest x1 227 us: gradients(): pl.pallas_call(kernel, out_shape=jax.ShapeDtypeStruct((6, D, FF), BF16),...]
    dot_general x15 -> x0, matrix products: 199 us -> none  [the longest x5 75.1 us: layer(): gate = jnp.dot(a, w['w_gate'], preferred_element_type=jnp.float32)]
    convert_element_type x2 -> x0, other arithmetic: 57.1 us -> none  [adamw(): return ((w - 0.02 * step).astype(jnp.bfloat16), m, v)]
    unnamed x40 -> x0, local copies, waits for them, and re-layouts: 9.26 us -> none
  transfers between devices with their start and end apart: 1 -> 0, of which waited for: 1 -> 0; matrix products, arithmetic and copies ran while one was open for 0% -> 0% of each run, Pallas kernels for 0% -> 0%
where the time goes in v2:
time: 283 us
  Pallas kernels  282 us (100%)
    pallas_call x1, Pallas kernels, gradients(): pl.pallas_call(kernel, out_shape=jax.ShapeDtypeStruct((6, D, FF), BF16),...  227 us
    pallas_call x1, Pallas kernels, optimizer(): pl.pallas_call(adamw_kernel, grid=(2, steps), out_shape=shapes, in_specs=...  55.2 us

profile of v2, /device:TPU:0, one launch (start us, length us, event | category | flops | bytes accessed | tf_op | source)
XLA Modules:
  0.0 282.8 jit_solution(9241068362963348700)
XLA Ops:
  0.6 226.9 %backward_sum.1.refs_0_.refs_1_.refs_2_ = bf16[6,640,2048]{2,1,0:T(8,128)(2,1)} custom-call(bf16[2048,640]{1,0:T(8,128)(2,1)} %bitcast.2, bf16[2048,640]{1,0:T(8,128)(2,1)} %bitcast.3, bf16[2,640,2048]{2,1,0:T(8,128)(2,1)} %refs_3_.1, bf16[2,640,2048]{2,1,0:T(8,128)(2,1)} %refs_4_.1, bf16[2,2048,640]{2,1,0:T(8,128)(2,1)} %refs_5_.1), custom_call_target="tpu_custom_call" | custom-call | flops 95000002560 | bytes 62914560 | tf_op jit(solution)/shard_map/backward_sum/pallas_call | solution.py:337
  227.6 55.2 %adamw.1 = (bf16[2,640,2048]{2,1,0:T(8,128)(2,1)}, bf16[2,640,2048]{2,1,0:T(8,128)(2,1)}, bf16[2,2048,640]{2,1,0:T(8,128)(2,1)}, f32[2,640,2048]{2,1,0:T(8,128)}...) custom-call(bf16[6,640,2048]{2,1,0:T(8,128)(2,1)} %backward_sum.1.re, ...), custom_call_target="tpu_custom_call" | custom-call | flops 120000000 | bytes 173000000 | tf_op jit(solution)/shard_map/adamw/pallas_call | solution.py:401

commit v3 on v2

--- a/solution.py
+++ b/solution.py
@@ -17,7 +17,7 @@
 HALF = D // 2
 PIECE = HALF // PARTS
 ROWS = 512
-FROWS = 512
+FROWS = 2048
 NROWS = 256
 F32, BF16 = jnp.float32, jnp.bfloat16
 MESH = pl.DeviceIdType.MESH
@@ -36,7 +36,7 @@
     return (w - 0.02 * step).astype(BF16), m, v
 
 
-AFTER = (2, 5, 8, 11, 13, 14)
+AFTER = (1, 4, 7, 10, 12, 13)
 
 
 def dot_t(a, b):

time: 283 us -> 281 us (level)
  no operation moved by 1% of the time
where the time goes in v3:
time: 281 us
  Pallas kernels  280 us (100%)
    pallas_call x1, Pallas kernels, gradients(): pl.pallas_call(kernel, out_shape=jax.ShapeDtypeStruct((6, D, FF), BF16),...  225 us
    pallas_call x1, Pallas kernels, optimizer(): pl.pallas_call(adamw_kernel, grid=(2, steps), out_shape=shapes, in_specs=...  55.2 us

profile of v3, /device:TPU:0, one launch (start us, length us, event | category | flops | bytes accessed | tf_op | source)
XLA Modules:
  0.0 281.0 jit_solution(10778296732089850344)
XLA Ops:
  0.6 225.1 %backward_sum.1.refs_0_.refs_1_.refs_2_ = bf16[6,640,2048]{2,1,0:T(8,128)(2,1)} custom-call(bf16[2048,640]{1,0:T(8,128)(2,1)} %bitcast.2, bf16[2048,640]{1,0:T(8,128)(2,1)} %bitcast.3, bf16[2,640,2048]{2,1,0:T(8,128)(2,1)} %refs_3_.1, bf16[2,640,2048]{2,1,0:T(8,128)(2,1)} %refs_4_.1, bf16[2,2048,640]{2,1,0:T(8,128)(2,1)} %refs_5_.1), custom_call_target="tpu_custom_call" | custom-call | flops 95000002560 | bytes 62914560 | tf_op jit(solution)/shard_map/backward_sum/pallas_call | solution.py:337
  225.8 55.2 %adamw.1 = (bf16[2,640,2048]{2,1,0:T(8,128)(2,1)}, bf16[2,640,2048]{2,1,0:T(8,128)(2,1)}, bf16[2,2048,640]{2,1,0:T(8,128)(2,1)}, f32[2,640,2048]{2,1,0:T(8,128)}...) custom-call(bf16[6,640,2048]{2,1,0:T(8,128)(2,1)} %backward_sum.1.re, ...), custom_call_target="tpu_custom_call" | custom-call | flops 120000000 | bytes 173000000 | tf_op jit(solution)/shard_map/adamw/pallas_call | solution.py:401
